TPU v7x, 32 devices: a whole 2x2x4 slice. The times are simulated.
32 devices in a mesh: row: 8 (over z, y), col: 4 (over x, core).
Axes of the slice: x: 2, y: 2, z: 4, core: 2. Of those that a mesh axis runs over, the one named last changes fastest.
Arguments:
- layer_input: bfloat16 [2048, 8192], P('row'), may hold values from -7 to 7
- gain: float32 [8192], replicated, may hold values from 0.5 to 6
- d_query: bfloat16 [2048, 4096], P('row', 'col'), may hold values from -6 to 6
- d_keyval: bfloat16 [2048, 2048], P('row', 'col'), may hold values from -6 to 6
- w_query: bfloat16 [8192, 4096], P('row', 'col'), may hold values from -0.0625 to 0.0625
- w_keyval: bfloat16 [8192, 2048], P('row', 'col'), may hold values from -1 to 1
- d_resid: bfloat16 [2048, 8192], P('row', 'col'), may hold values from -6 to 6
Outputs:
- d_input: bfloat16 [2048, 8192], P('row', 'col')
- grad_wq: bfloat16 [8192, 4096], P('row', 'col')
- grad_wkv: bfloat16 [8192, 2048], P('row', 'col')
- grad_gain: float32 [8192], P('col')
- grad_square_sum: float32 [], replicated
All inputs are finite; a program needn't handle non-finite values.
Results may differ from a plain program's by a relative error of at most 0.023.
Values may be sent and summed in bfloat16 or wider, within the bound.
A program may use at most 128 MiB of HBM per device.

v0:
```python
import math
import jax
import jax.numpy as jnp
from jax import lax
from jax.sharding import PartitionSpec as P

epsilon = 1e-05


def local(layer_input, gain, d_query, d_keyval, w_query, w_keyval, d_resid):
    inputs = layer_input.astype(jnp.float32)
    inv_rms = lax.rsqrt(jnp.mean(inputs * inputs, axis=1, keepdims=True) + epsilon)
    normed = (inputs * inv_rms * gain).astype(jnp.bfloat16)
    model_width = inputs.shape[1]
    local_tokens = inputs.shape[0]
    tokens_all = local_tokens * lax.axis_size("row")
    scaling = 1.0 / math.sqrt(tokens_all)
    weight_scale = 1.0 / math.sqrt(local_tokens)
    contract_cols = (((1,), (1,)), ((), ()))
    partial_value = lax.dot_general(
        d_query,
        lax.all_gather(w_query, "row", axis=0, tiled=True),
        contract_cols,
        preferred_element_type=jnp.float32,
    )
    partial_value = partial_value + lax.dot_general(
        d_keyval,
        lax.all_gather(w_keyval, "row", axis=0, tiled=True),
        contract_cols,
        preferred_element_type=jnp.float32,
    )
    rounded = lax.optimization_barrier(partial_value.astype(jnp.bfloat16)).astype(jnp.float32)
    feature_grad = lax.psum_scatter(
        rounded.astype(jnp.bfloat16), "col", scatter_dimension=1, tiled=True
    ).astype(jnp.float32)
    slice_width = feature_grad.shape[1]
    col_start = lax.axis_index("col") * slice_width
    input_part = lax.dynamic_slice_in_dim(inputs, col_start, slice_width, 1)
    gain_part = lax.dynamic_slice_in_dim(gain, col_start, slice_width, 0)
    weighted = gain_part * feature_grad
    token_dot = lax.psum(jnp.sum(weighted * input_part, axis=1, keepdims=True), "col")
    d_input = (
        d_resid.astype(jnp.float32)
        + inv_rms * weighted
        - input_part * inv_rms**3 * token_dot / model_width
    ).astype(jnp.bfloat16)
    gain_partial = jnp.sum(feature_grad * input_part * inv_rms, axis=0) * scaling
    cotangent = jnp.concatenate([d_query, d_keyval], axis=1)
    query_cols = d_query.shape[1]
    columns = lax.all_to_all(normed, "row", split_axis=1, concat_axis=0, tiled=True)
    all_cotangents = lax.all_gather(cotangent, "row", axis=0, tiled=True)
    groups = lax.axis_size("row")
    column_blocks = columns.reshape(groups, local_tokens, columns.shape[1])
    grad_blocks = all_cotangents.reshape(groups, local_tokens, all_cotangents.shape[1])
    blocks = (
        lax.dot_general(
            column_blocks,
            grad_blocks,
            (((1,), (1,)), ((0,), (0,))),
            preferred_element_type=jnp.float32,
        )
        * weight_scale
    )
    summed = jnp.sum(blocks.astype(jnp.bfloat16).astype(jnp.float32), axis=0)
    grad_wq = summed[:, :query_cols].astype(jnp.bfloat16)
    grad_wkv = summed[:, query_cols:].astype(jnp.bfloat16)
    query_f = grad_wq.astype(jnp.float32)
    keyval_f = grad_wkv.astype(jnp.float32)
    tile_square = jnp.sum(query_f * query_f) + jnp.sum(keyval_f * keyval_f)
    grad_gain = lax.psum(gain_partial, "row")
    leading = jnp.where(
        lax.axis_index("row") == 0, jnp.sum(grad_gain * grad_gain), jnp.float32(0.0)
    )
    grand_total = lax.psum(tile_square + leading, ("row", "col"))
    grad_square_sum = grand_total / jnp.float32(model_width)
    return (d_input, grad_wq, grad_wkv, grad_gain, grad_square_sum)


def solution(mesh):
    placed = (
        P("row", None),
        P(),
        P("row", "col"),
        P("row", "col"),
        P("row", "col"),
        P("row", "col"),
        P("row", "col"),
    )
    return jax.shard_map(
        local,
        mesh=mesh,
        in_specs=placed,
        out_specs=(P("row", "col"), P("row", "col"), P("row", "col"), P("col"), P()),
        check_vma=False,
    )
```

profile of v0, /device:TPU:12, one launch (start us, length us, event | category | flops | bytes accessed | tf_op | source)
XLA Modules:
  0.0 671.1 jit_solution(14180824158022452798)
XLA Ops:
  7.2 0.7 all-gather.6.cloned.1.call-update
  8.0 0.7 all-gather.4.cloned.1.call-update
  8.7 2.1 pad_maximum_fusion
  10.8 3.3 multiply_reduce_fusion
  14.1 0.2 copy-done
  14.2 3.2 multiply_convert_fusion.1
  17.4 6.5 copy.13
  23.9 6.4 all-to-all-start
  30.3 181.7 %all-gather.6.cloned.1.call-done = bf16[8192,512]{1,0:T(8,128)(2,1)} async-done(((bf16[1024,512]{1,0:T(8,128)(2,1)}), bf16[8192,512]{1,0:T(8,128)(2,1)}) %all-gather.6.cloned.1.call-update) | async-done | bytes 8388624 | tf_op jit(solution)/shard_map/all_gather | solution.py:28
  212.1 9.0 %fusion.11 = f32[256,8192]{1,0:T(8,128)} fusion(bf16[256,512]{1,0:T(8,128)(2,1)S(1)} %copy-done.2, bf16[8192,512]{1,0:T(8,128)(2,1)} %all-gather.6.cloned.1.call-done), kind=kOutput, calls=%fused_computation.24 | convolution fusion | flops 2147483648 | bytes 17039360 | tf_op jit(solution)/shard_map/dot_general | solution.py:26
  221.0 219.9 %all-gather.4.cloned.1.call-done = bf16[8192,1024]{1,0:T(8,128)(2,1)} async-done(((bf16[1024,1024]{1,0:T(8,128)(2,1)}), bf16[8192,1024]{1,0:T(8,128)(2,1)}) %all-gather.4.cloned.1.call-update) | async-done | bytes 16777232 | tf_op jit(solution)/shard_map/all_gather | solution.py:22
  440.9 12.4 %fusion = bf16[256,8192]{1,0:T(8,128)(2,1)} fusion(f32[256,8192]{1,0:T(8,128)} %fusion.11, bf16[256,1024]{1,0:T(8,128)(2,1)S(1)} %copy-done.1, bf16[8192,1024]{1,0:T(8,128)(2,1)} %all-gather.4.cloned.1.call-done), kind=kOutput, calls=%fused_computation.2 | convolution fusion | flops 4299161600 | bytes 29884416 | tf_op jit(solution)/shard_map/dot_general | solution.py:20
  453.4 6.7 convert_element_type.35
  460.0 81.3 %all-gather.8.cloned.1.call-done = bf16[2048,1536]{1,0:T(8,128)(2,1)} async-done(((bf16[256,1536]{1,0:T(8,128)(2,1)}), bf16[2048,1536]{1,0:T(8,128)(2,1)}) %all-gather.8.cloned.1.call-update) | async-done | bytes 6291472 | tf_op jit(solution)/shard_map/all_gather | solution.py:51
  541.3 10.9 %fusion.1 = bf16[1024,1536]{1,0:T(8,128)(2,1)S(1)} fusion(bf16[8,256,1536]{2,1,0:T(8,128)(2,1)} %bitcast.11, bf16[256,8,1024]{0,2,1:T(8,128)(2,1)} %all-to-all-done), kind=kOutput, calls=%fused_computation.5 | convolution fusion | flops 6478626816 | bytes 13631488 | tf_op jit(solution)/shard_map/dot_general | solution.py:56
  552.2 2.0 multiply_reduce_fusion.2
  554.3 2.9 multiply_reduce_fusion.1
  558.5 29.9 %reduce-scatter.2.cloned.1.call-done = bf16[256,2048]{1,0:T(8,128)(2,1)} async-done(((bf16[256,8192]{1,0:T(8,128)(2,1)}), bf16[256,2048]{1,0:T(8,128)(2,1)}) %reduce-scatter.2.cloned.1.call-update) | async-done | bytes 1048592 | tf_op jit(solution)/shard_map/reduce_scatter | solution.py:33
  588.4 2.6 fusion.10
  591.0 15.3 %psum.22 = f32[2048]{0:T(1024)S(1)} all-reduce(f32[2048]{0:T(1024)S(1)} %broadcast_multiply_fusion), channel_id=1, replica_groups=mesh['row'=8,'col'=4] {'row'}, use_global_device_ids=true, to_apply=%region_6.0 | all-reduce | flops 2048 | bytes 16384 | tf_op jit(solution)/shard_map/psum | solution.py:70
  606.3 0.6 multiply_reduce_fusion.3
  607.5 6.0 psum.21
  613.5 45.6 %psum.23 = f32[]{:T(128)} all-reduce(f32[]{:T(128)S(6)} %add.44), channel_id=1, replica_groups=mesh['row'=8,'col'=4] {'row','col'}, use_global_device_ids=true, to_apply=%region_10.11 | all-reduce | flops 1 | bytes 8 | tf_op jit(solution)/shard_map/psum | solution.py:74
  659.8 3.6 fusion.7
  (21 shorter events, 0.2 us)
Async XLA Ops:
  7.2 204.9 %all-gather.6.cloned.1.call-start = ((), (), s32[]{:S(2)}) async-start(), calls=%async_computation.3 | async-start | bytes 9437184 | tf_op jit(solution)/shard_map/all_gather | solution.py:28
  7.9 6.2 copy-start.4
  7.9 433.0 %all-gather.4.cloned.1.call-start = ((), (), s32[]{:S(2)}) async-start(), calls=%async_computation.2 | async-start | bytes 18874368 | tf_op jit(solution)/shard_map/all_gather | solution.py:22
  8.7 532.6 %all-gather.8.cloned.1.call-start = ((), (), s32[]{:S(2)}) async-start(), calls=%async_computation.5 | async-start | bytes 7077888 | tf_op jit(solution)/shard_map/all_gather | solution.py:51
  10.8 3.5 copy-start
  23.9 188.1 %copy-start.2 = (bf16[256,512]{1,0:T(8,128)(2,1)S(1)}, bf16[256,512]{1,0:T(8,128)(2,1)}, u32[]{:S(2)}) copy-start(bf16[256,512]{1,0:T(8,128)(2,1)} %param.10) | copy-start | bytes 786436
  23.9 436.1 %all-to-all-start = ((bf16[256,8,1024]{0,2,1:T(8,128)(2,1)}), bf16[256,8,1024]{0,2,1:T(8,128)(2,1)}, u32[]{:S(2)}, u32[]{:S(2)}) async-start(bf16[256,8,1024]{0,2,1:T(8,128)(2,1)} %bitcast.10), calls=%async_computation.1 | async-start | bytes 8388608 | tf_op jit(solution)/shard_map/all_to_all | solution.py:50
  30.3 410.6 %copy-start.1 = (bf16[256,1024]{1,0:T(8,128)(2,1)S(1)}, bf16[256,1024]{1,0:T(8,128)(2,1)}, u32[]{:S(2)}) copy-start(bf16[256,1024]{1,0:T(8,128)(2,1)} %param.9) | copy-start | bytes 1572868
  30.3 558.1 %reduce-scatter.2.cloned.1.call-start = ((), (), s32[]{:S(2)}) async-start(), calls=%async_computation.4 | async-start | bytes 5242880 | tf_op jit(solution)/shard_map/reduce_scatter | solution.py:33
  554.3 105.5 %copy-start.3 = (bf16[256,2048]{1,0:T(8,128)(2,1)S(1)}, bf16[256,2048]{1,0:T(8,128)(2,1)}, u32[]{:S(2)}) copy-start(bf16[256,2048]{1,0:T(8,128)(2,1)} %param.13) | copy-start | bytes 3145732
  606.3 57.1 %copy-start.5 = (f32[2048]{0:T(1024)}, f32[2048]{0:T(1024)S(1)}, u32[]{:S(2)}) copy-start(f32[2048]{0:T(1024)S(1)} %psum.22) | copy-start | bytes 24580
Sparse Core Ops, SparseCore 0:
  10.1 201.9 all-gather.5
  214.2 226.7 all-gather.3
  443.7 97.5 all-gather.7
  543.7 44.6 reduce-scatter.1
where the time goes:
time: 672 us; the launch traced here: 671 us
  waiting for transfers between devices  514 us (76%)
  blocking collectives  66.8 us (10%)
  matrix products  32.3 us (5%)
  other arithmetic  27 us (4%)
  between operations  17.6 us (3%)
    all_gather x1, waiting for transfers between devices, local(): lax.all_gather(w_query, 'row', axis=0, tiled=True)  220 us
    all_gather x1, waiting for transfers between devices, local(): lax.all_gather(w_keyval, 'row', axis=0, tiled=True)  182 us
    all_gather x1, waiting for transfers between devices, local(): all_cotangents = lax.all_gather(cotangent, 'row', axis=0, tiled=True)  81.3 us
    psum x1, blocking collectives, local(): grand_total = lax.psum(tile_square + leading, ('row', 'col'))  45.6 us
    reduce_scatter x1, waiting for transfers between devices, local(): lax.psum_scatter(rounded.astype(jnp.bfloat16), 'col', scatter_dimension=1...  29.9 us
    psum x1, blocking collectives, local(): grad_gain = lax.psum(gain_partial, 'row')  15.3 us
  transfers between devices with their start and end apart: 5, of which 4 were waited for; matrix products, arithmetic and copies ran while one was open for 9% of the time, Pallas kernels for 0%

commit v1 on v0

--- a/solution.py
+++ b/solution.py
@@ -71,7 +71,9 @@
     leading = jnp.where(
         lax.axis_index("row") == 0, jnp.sum(grad_gain * grad_gain), jnp.float32(0.0)
     )
-    grand_total = lax.psum(tile_square + leading, ("row", "col"))
+    x = tile_square + leading
+    parts = lax.all_gather(x, ("row", "col"), axis=0, tiled=False)
+    grand_total = parts.sum(axis=0)
     grad_square_sum = grand_total / jnp.float32(model_width)
     return (d_input, grad_wq, grad_wkv, grad_gain, grad_square_sum)
 

time: 672 us -> 672 us (level)
    psum x1 -> x0, blocking collectives: 45.6 us -> none  [local(): grand_total = lax.psum(tile_square + leading, ('row', 'col'))]
    unnamed x0 -> x1, blocking collectives: none -> 45.4 us
where the time goes in v1:
time: 672 us
  waiting for transfers between devices  514 us (76%)
  blocking collectives  66.6 us (10%)
  matrix products  32.3 us (5%)
  other arithmetic  27.6 us (4%)
  between operations  17.6 us (3%)
  local copies, waits for them, and re-layouts  6.81 us (1%)
    all_gather x1, waiting for transfers between devices, local(): lax.all_gather(w_query, 'row', axis=0, tiled=True)  220 us
    all_gather x1, waiting for transfers between devices, local(): lax.all_gather(w_keyval, 'row', axis=0, tiled=True)  182 us
    all_gather x1, waiting for transfers between devices, local(): all_cotangents = lax.all_gather(cotangent, 'row', axis=0, tiled=True)  81.3 us
    unnamed x1, blocking collectives  45.4 us
    reduce_scatter x1, waiting for transfers between devices, local(): lax.psum_scatter(rounded.astype(jnp.bfloat16), 'col', scatter_dimension=1...  29.9 us
    psum x1, blocking collectives, local(): grad_gain = lax.psum(gain_partial, 'row')  15.3 us
  transfers between devices with their start and end apart: 5, of which 4 were waited for; matrix products, arithmetic and copies ran while one was open for 9% of the time, Pallas kernels for 0%

profile of v1, /device:TPU:12, one launch (start us, length us, event | category | flops | bytes accessed | tf_op | source)
XLA Modules:
  0.0 671.6 jit_solution(4827487894507442577)
XLA Ops:
  7.2 0.7 all-gather.6.cloned.1.call-update
  8.0 0.7 all-gather.4.cloned.1.call-update
  8.7 2.1 pad_maximum_fusion
  10.8 3.3 multiply_reduce_fusion
  14.2 3.2 multiply_convert_fusion.1
  17.4 6.5 copy.13
  23.9 6.4 all-to-all-start
  30.3 181.7 %all-gather.6.cloned.1.call-done = bf16[8192,512]{1,0:T(8,128)(2,1)} async-done(((bf16[1024,512]{1,0:T(8,128)(2,1)}), bf16[8192,512]{1,0:T(8,128)(2,1)}) %all-gather.6.cloned.1.call-update) | async-done | bytes 8388624 | tf_op jit(solution)/shard_map/all_gather | solution.py:28
  212.1 9.0 %fusion.11 = f32[256,8192]{1,0:T(8,128)} fusion(bf16[256,512]{1,0:T(8,128)(2,1)S(1)} %copy-done.2, bf16[8192,512]{1,0:T(8,128)(2,1)} %all-gather.6.cloned.1.call-done), kind=kOutput, calls=%fused_computation.24 | convolution fusion | flops 2147483648 | bytes 17039360 | tf_op jit(solution)/shard_map/dot_general | solution.py:26
  221.0 219.9 %all-gather.4.cloned.1.call-done = bf16[8192,1024]{1,0:T(8,128)(2,1)} async-done(((bf16[1024,1024]{1,0:T(8,128)(2,1)}), bf16[8192,1024]{1,0:T(8,128)(2,1)}) %all-gather.4.cloned.1.call-update) | async-done | bytes 16777232 | tf_op jit(solution)/shard_map/all_gather | solution.py:22
  440.9 12.4 %fusion = bf16[256,8192]{1,0:T(8,128)(2,1)} fusion(f32[256,8192]{1,0:T(8,128)} %fusion.11, bf16[256,1024]{1,0:T(8,128)(2,1)S(1)} %copy-done.1, bf16[8192,1024]{1,0:T(8,128)(2,1)} %all-gather.4.cloned.1.call-done), kind=kOutput, calls=%fused_computation.2 | convolution fusion | flops 4299161600 | bytes 29884416 | tf_op jit(solution)/shard_map/dot_general | solution.py:20
  453.4 6.7 convert_element_type.35
  460.0 81.3 %all-gather.8.cloned.1.call-done = bf16[2048,1536]{1,0:T(8,128)(2,1)} async-done(((bf16[256,1536]{1,0:T(8,128)(2,1)}), bf16[2048,1536]{1,0:T(8,128)(2,1)}) %all-gather.8.cloned.1.call-update) | async-done | bytes 6291472 | tf_op jit(solution)/shard_map/all_gather | solution.py:51
  541.3 10.9 %fusion.1 = bf16[1024,1536]{1,0:T(8,128)(2,1)S(1)} fusion(bf16[8,256,1536]{2,1,0:T(8,128)(2,1)} %bitcast.12, bf16[256,8,1024]{0,2,1:T(8,128)(2,1)} %all-to-all-done), kind=kOutput, calls=%fused_computation.5 | convolution fusion | flops 6478626816 | bytes 13631488 | tf_op jit(solution)/shard_map/dot_general | solution.py:56
  552.2 2.0 multiply_reduce_fusion.2
  554.3 2.9 multiply_reduce_fusion.1
  558.5 29.9 %reduce-scatter.2.cloned.1.call-done = bf16[256,2048]{1,0:T(8,128)(2,1)} async-done(((bf16[256,8192]{1,0:T(8,128)(2,1)}), bf16[256,2048]{1,0:T(8,128)(2,1)}) %reduce-scatter.2.cloned.1.call-update) | async-done | bytes 1048592 | tf_op jit(solution)/shard_map/reduce_scatter | solution.py:33
  588.4 2.6 fusion.10
  591.0 15.3 %psum.15 = f32[2048]{0:T(1024)S(1)} all-reduce(f32[2048]{0:T(1024)S(1)} %broadcast_multiply_fusion), channel_id=1, replica_groups=mesh['row'=8,'col'=4] {'row'}, use_global_device_ids=true, to_apply=%region_6.0 | all-reduce | flops 2048 | bytes 16384 | tf_op jit(solution)/shard_map/psum | solution.py:70
  606.3 0.6 multiply_reduce_fusion.3
  607.6 5.9 psum.14
  613.6 45.4 %all-reduce = f32[32]{0:T(128)S(1)} all-reduce(f32[32]{0:T(128)S(1)} %dynamic-update-slice), channel_id=1, replica_groups=mesh['row'=8,'col'=4] {'row','col'}, use_global_device_ids=true, to_apply=%add | all-reduce | flops 32 | bytes 256
  659.0 0.6 reduce_sum.79
  660.2 3.6 fusion.7
  (24 shorter events, 0.5 us)
Async XLA Ops:
  7.2 204.9 %all-gather.6.cloned.1.call-start = ((), (), s32[]{:S(2)}) async-start(), calls=%async_computation.3 | async-start | bytes 9437184 | tf_op jit(solution)/shard_map/all_gather | solution.py:28
  7.9 6.2 copy-start.4
  7.9 433.0 %all-gather.4.cloned.1.call-start = ((), (), s32[]{:S(2)}) async-start(), calls=%async_computation.2 | async-start | bytes 18874368 | tf_op jit(solution)/shard_map/all_gather | solution.py:22
  8.7 532.6 %all-gather.8.cloned.1.call-start = ((), (), s32[]{:S(2)}) async-start(), calls=%async_computation.5 | async-start | bytes 7077888 | tf_op jit(solution)/shard_map/all_gather | solution.py:51
  10.8 3.5 copy-start
  23.9 188.1 %copy-start.2 = (bf16[256,512]{1,0:T(8,128)(2,1)S(1)}, bf16[256,512]{1,0:T(8,128)(2,1)}, u32[]{:S(2)}) copy-start(bf16[256,512]{1,0:T(8,128)(2,1)} %param.10) | copy-start | bytes 786436
  23.9 436.1 %all-to-all-start = ((bf16[256,8,1024]{0,2,1:T(8,128)(2,1)}), bf16[256,8,1024]{0,2,1:T(8,128)(2,1)}, u32[]{:S(2)}, u32[]{:S(2)}) async-start(bf16[256,8,1024]{0,2,1:T(8,128)(2,1)} %bitcast.11), calls=%async_computation.1 | async-start | bytes 8388608 | tf_op jit(solution)/shard_map/all_to_all | solution.py:50
  30.3 410.6 %copy-start.1 = (bf16[256,1024]{1,0:T(8,128)(2,1)S(1)}, bf16[256,1024]{1,0:T(8,128)(2,1)}, u32[]{:S(2)}) copy-start(bf16[256,1024]{1,0:T(8,128)(2,1)} %param.9) | copy-start | bytes 1572868
  30.3 558.1 %reduce-scatter.2.cloned.1.call-start = ((), (), s32[]{:S(2)}) async-start(), calls=%async_computation.4 | async-start | bytes 5242880 | tf_op jit(solution)/shard_map/reduce_scatter | solution.py:33
  554.3 106.0 %copy-start.3 = (bf16[256,2048]{1,0:T(8,128)(2,1)S(1)}, bf16[256,2048]{1,0:T(8,128)(2,1)}, u32[]{:S(2)}) copy-start(bf16[256,2048]{1,0:T(8,128)(2,1)} %param.13) | copy-start | bytes 3145732
  606.3 57.6 %copy-start.5 = (f32[2048]{0:T(1024)}, f32[2048]{0:T(1024)S(1)}, u32[]{:S(2)}) copy-start(f32[2048]{0:T(1024)S(1)} %psum.15) | copy-start | bytes 24580
Sparse Core Ops, SparseCore 0:
  10.1 201.9 all-gather.5
  214.2 226.7 all-gather.3
  443.7 97.5 all-gather.7
  543.7 44.6 reduce-scatter.1

commit v2 on v0

--- a/solution.py
+++ b/solution.py
@@ -71,7 +71,8 @@
     leading = jnp.where(
         lax.axis_index("row") == 0, jnp.sum(grad_gain * grad_gain), jnp.float32(0.0)
     )
-    grand_total = lax.psum(tile_square + leading, ("row", "col"))
+    one_axis = lax.psum(tile_square + leading, "row")
+    grand_total = lax.psum(one_axis, "col")
     grad_square_sum = grand_total / jnp.float32(model_width)
     return (d_input, grad_wq, grad_wkv, grad_gain, grad_square_sum)
 

time: 672 us -> 652 us (0.970)
  blocking collectives: 66.8 us -> 43.7 us
    psum x1, blocking collectives: 45.6 us -> 21.9 us  [local(): one_axis = lax.psum(tile_square + leading, 'row')]
where the time goes in v2:
time: 652 us; the launch traced here: 648 us
  waiting for transfers between devices  514 us (79%)
  blocking collectives  43.7 us (7%)
  matrix products  32.3 us (5%)
  other arithmetic  27 us (4%)
  between operations  17.6 us (3%)
  local copies, waits for them, and re-layouts  6.69 us (1%)
    all_gather x1, waiting for transfers between devices, local(): lax.all_gather(w_query, 'row', axis=0, tiled=True)  220 us
    all_gather x1, waiting for transfers between devices, local(): lax.all_gather(w_keyval, 'row', axis=0, tiled=True)  182 us
    all_gather x1, waiting for transfers between devices, local(): all_cotangents = lax.all_gather(cotangent, 'row', axis=0, tiled=True)  81.3 us
    reduce_scatter x1, waiting for transfers between devices, local(): lax.psum_scatter(rounded.astype(jnp.bfloat16), 'col', scatter_dimension=1...  29.9 us
    psum x1, blocking collectives, local(): one_axis = lax.psum(tile_square + leading, 'row')  21.9 us
    psum x1, blocking collectives, local(): grad_gain = lax.psum(gain_partial, 'row')  15.3 us
  transfers between devices with their start and end apart: 5, of which 4 were waited for; matrix products, arithmetic and copies ran while one was open for 9% of the time, Pallas kernels for 0%

profile of v2, /device:TPU:12, one launch (start us, length us, event | category | flops | bytes accessed | tf_op | source)
XLA Modules:
  0.0 647.9 jit_solution(7471728717102436733)
XLA Ops:
  7.2 0.7 all-gather.6.cloned.1.call-update
  8.0 0.7 all-gather.4.cloned.1.call-update
  8.7 2.1 pad_maximum_fusion
  10.8 3.3 multiply_reduce_fusion
  14.1 0.2 copy-done
  14.2 3.2 multiply_convert_fusion.1
  17.4 6.5 %copy.13 = bf16[256,8192]{0,1:T(8,128)(2,1)} copy(bf16[256,8192]{1,0:T(8,128)(2,1)} %multiply_convert_fusion.1) | data formatting | bytes 8388608 | tf_op jit(solution)/shard_map/all_to_all | solution.py:50
  23.9 6.4 all-to-all-start
  30.3 181.7 %all-gather.6.cloned.1.call-done = bf16[8192,512]{1,0:T(8,128)(2,1)} async-done(((bf16[1024,512]{1,0:T(8,128)(2,1)}), bf16[8192,512]{1,0:T(8,128)(2,1)}) %all-gather.6.cloned.1.call-update) | async-done | bytes 8388624 | tf_op jit(solution)/shard_map/all_gather | solution.py:28
  212.0 9.0 %fusion.11 = f32[256,8192]{1,0:T(8,128)} fusion(bf16[256,512]{1,0:T(8,128)(2,1)S(1)} %copy-done.2, bf16[8192,512]{1,0:T(8,128)(2,1)} %all-gather.6.cloned.1.call-done), kind=kOutput, calls=%fused_computation.24 | convolution fusion | flops 2147483648 | bytes 17039360 | tf_op jit(solution)/shard_map/dot_general | solution.py:26
  221.0 219.9 %all-gather.4.cloned.1.call-done = bf16[8192,1024]{1,0:T(8,128)(2,1)} async-done(((bf16[1024,1024]{1,0:T(8,128)(2,1)}), bf16[8192,1024]{1,0:T(8,128)(2,1)}) %all-gather.4.cloned.1.call-update) | async-done | bytes 16777232 | tf_op jit(solution)/shard_map/all_gather | solution.py:22
  440.9 12.4 %fusion = bf16[256,8192]{1,0:T(8,128)(2,1)} fusion(f32[256,8192]{1,0:T(8,128)} %fusion.11, bf16[256,1024]{1,0:T(8,128)(2,1)S(1)} %copy-done.1, bf16[8192,1024]{1,0:T(8,128)(2,1)} %all-gather.4.cloned.1.call-done), kind=kOutput, calls=%fused_computation.2 | convolution fusion | flops 4299161600 | bytes 29884416 | tf_op jit(solution)/shard_map/dot_general | solution.py:20
  453.4 6.7 %convert_element_type.35 = f32[256,8192]{1,0:T(8,128)} convert(bf16[256,8192]{1,0:T(8,128)(2,1)} %param.7) | non-fusion elementwise | flops 2097152 | bytes 12582912 | tf_op jit(solution)/shard_map/convert_element_type | solution.py:11
  460.1 81.3 %all-gather.8.cloned.1.call-done = bf16[2048,1536]{1,0:T(8,128)(2,1)} async-done(((bf16[256,1536]{1,0:T(8,128)(2,1)}), bf16[2048,1536]{1,0:T(8,128)(2,1)}) %all-gather.8.cloned.1.call-update) | async-done | bytes 6291472 | tf_op jit(solution)/shard_map/all_gather | solution.py:51
  541.3 10.9 %fusion.1 = bf16[1024,1536]{1,0:T(8,128)(2,1)S(1)} fusion(bf16[8,256,1536]{2,1,0:T(8,128)(2,1)} %bitcast.11, bf16[256,8,1024]{0,2,1:T(8,128)(2,1)} %all-to-all-done), kind=kOutput, calls=%fused_computation.5 | convolution fusion | flops 6478626816 | bytes 13631488 | tf_op jit(solution)/shard_map/dot_general | solution.py:56
  552.2 2.0 multiply_reduce_fusion.2
  554.3 2.9 multiply_reduce_fusion.1
  558.5 29.9 %reduce-scatter.2.cloned.1.call-done = bf16[256,2048]{1,0:T(8,128)(2,1)} async-done(((bf16[256,8192]{1,0:T(8,128)(2,1)}), bf16[256,2048]{1,0:T(8,128)(2,1)}) %reduce-scatter.2.cloned.1.call-update) | async-done | bytes 1048592 | tf_op jit(solution)/shard_map/reduce_scatter | solution.py:33
  588.4 2.6 fusion.10
  591.0 15.3 %psum.29 = f32[2048]{0:T(1024)S(1)} all-reduce(f32[2048]{0:T(1024)S(1)} %broadcast_multiply_fusion), channel_id=1, replica_groups=mesh['row'=8,'col'=4] {'row'}, use_global_device_ids=true, to_apply=%region_6.0 | all-reduce | flops 2048 | bytes 16384 | tf_op jit(solution)/shard_map/psum | solution.py:70
  606.3 0.6 multiply_reduce_fusion.3
  607.5 21.9 %psum.30 = f32[]{:T(128)} all-reduce(f32[]{:T(128)S(6)} %add.46), channel_id=1, replica_groups=mesh['row'=8,'col'=4] {'row'}, use_global_device_ids=true, to_apply=%region_10.11 | all-reduce | flops 1 | bytes 8 | tf_op jit(solution)/shard_map/psum | solution.py:74
  629.4 6.5 %all-reduce = (f32[256]{0:T(256)S(1)}, f32[]{:T(128)}) all-reduce(f32[256]{0:T(256)S(1)} %get-tuple-element.6, f32[]{:T(128)} %psum.30), channel_id=1, replica_groups=mesh['row'=8,'col'=4] {'col'}, use_global_device_ids=true, to_apply=%region_3.0 | all-reduce | flops 257 | bytes 2056 | tf_op jit(solution)/shard_map/psum | solution.py:41
  636.6 3.6 fusion.7
  (21 shorter events, 0.2 us)
Async XLA Ops:
  7.2 204.9 %all-gather.6.cloned.1.call-start = ((), (), s32[]{:S(2)}) async-start(), calls=%async_computation.3 | async-start | bytes 9437184 | tf_op jit(solution)/shard_map/all_gather | solution.py:28
  7.9 6.2 copy-start.4
  7.9 433.0 %all-gather.4.cloned.1.call-start = ((), (), s32[]{:S(2)}) async-start(), calls=%async_computation.2 | async-start | bytes 18874368 | tf_op jit(solution)/shard_map/all_gather | solution.py:22
  8.7 532.6 %all-gather.8.cloned.1.call-start = ((), (), s32[]{:S(2)}) async-start(), calls=%async_computation.5 | async-start | bytes 7077888 | tf_op jit(solution)/shard_map/all_gather | solution.py:51
  10.8 3.5 copy-start
  23.9 188.1 %copy-start.2 = (bf16[256,512]{1,0:T(8,128)(2,1)S(1)}, bf16[256,512]{1,0:T(8,128)(2,1)}, u32[]{:S(2)}) copy-start(bf16[256,512]{1,0:T(8,128)(2,1)} %param.10) | copy-start | bytes 786436
  23.9 436.1 %all-to-all-start = ((bf16[256,8,1024]{0,2,1:T(8,128)(2,1)}), bf16[256,8,1024]{0,2,1:T(8,128)(2,1)}, u32[]{:S(2)}, u32[]{:S(2)}) async-start(bf16[256,8,1024]{0,2,1:T(8,128)(2,1)} %bitcast.10), calls=%async_computation.1 | async-start | bytes 8388608 | tf_op jit(solution)/shard_map/all_to_all | solution.py:50
  30.3 410.6 %copy-start.1 = (bf16[256,1024]{1,0:T(8,128)(2,1)S(1)}, bf16[256,1024]{1,0:T(8,128)(2,1)}, u32[]{:S(2)}) copy-start(bf16[256,1024]{1,0:T(8,128)(2,1)} %param.9) | copy-start | bytes 1572868
  30.3 558.1 %reduce-scatter.2.cloned.1.call-start = ((), (), s32[]{:S(2)}) async-start(), calls=%async_computation.4 | async-start | bytes 5242880 | tf_op jit(solution)/shard_map/reduce_scatter | solution.py:33
  554.3 82.3 %copy-start.3 = (bf16[256,2048]{1,0:T(8,128)(2,1)S(1)}, bf16[256,2048]{1,0:T(8,128)(2,1)}, u32[]{:S(2)}) copy-start(bf16[256,2048]{1,0:T(8,128)(2,1)} %param.13) | copy-start | bytes 3145732
  606.3 34.0 %copy-start.5 = (f32[2048]{0:T(1024)}, f32[2048]{0:T(1024)S(1)}, u32[]{:S(2)}) copy-start(f32[2048]{0:T(1024)S(1)} %psum.29) | copy-start | bytes 24580
Sparse Core Ops, SparseCore 0:
  10.1 201.9 all-gather.5
  214.2 226.7 all-gather.3
  443.7 97.5 all-gather.7
  543.7 44.6 reduce-scatter.1
